TPU v7x, 256 devices: a whole 4x4x8 slice. The times are simulated.
256 devices in a mesh: pq: 8 (over z_hi, x), rs: 32 (over y, z_lo, core).
Axes of the slice: x: 4, y: 4, z: 8 (z_hi: 2, z_lo: 4; z = z_hi * 4 + z_lo), core: 2. Of those that a mesh axis runs over, the one named last changes fastest.
Arguments:
- integrals: bfloat16 [512, 1152, 1152], P('pq', 'rs'), may hold values from -6 to 6
- coeff: bfloat16 [1152, 896], P('rs', 'pq'), may hold values from -0.1875 to 0.1875
Outputs:
- half_mo: bfloat16 [512, 896, 896], P('pq', 'rs')
All inputs are finite; a program needn't handle non-finite values.
Results may differ from a plain program's by a relative error of at most 0.0049.
Values may be sent and summed in bfloat16 or wider, within the bound.
No kernel may reach another device: no remote copies, remote signals or barrier semaphores. Data moves between devices by JAX's collectives and lax.ppermute only.
A program may use at most 128 MiB of HBM per device.

v0:
```python
import jax
import jax.numpy as jnp
from jax import lax
from jax.sharding import PartitionSpec as P

NBASIS = 1152
NORB = 896


def joined_along(parts, dim):
    parts = jnp.moveaxis(parts, 0, dim)
    lengths = parts.shape
    return parts.reshape(*lengths[:dim], lengths[dim] * lengths[dim + 1], *lengths[dim + 2 :])


def from_everyone(array, axis):
    count = lax.axis_size(axis)
    return lax.all_to_all(
        jnp.broadcast_to(array[None], (count, *array.shape)), axis, 0, 0, tiled=True
    )


def collect(array, axis, dim):
    return joined_along(from_everyone(array, axis), dim)


def second_half(received, panel):
    return jnp.einsum("prl,rk->plk", received, panel, preferred_element_type=jnp.float32).astype(
        jnp.bfloat16
    )


def on_device(integrals, coeff):
    pair_rows = integrals.shape[0]
    block_rows = integrals.shape[1]
    flat = integrals.reshape(pair_rows * block_rows, NBASIS)
    strip = collect(coeff, "pq", 1)
    panel = collect(strip, "rs", 0)
    first = jnp.dot(flat, panel, preferred_element_type=jnp.float32).astype(jnp.bfloat16)
    first = first.reshape(pair_rows, block_rows, NORB)
    return second_half(lax.all_to_all(first, "rs", split_axis=2, concat_axis=1, tiled=True), panel)


def solution(mesh):
    placed = (P("pq", "rs", None), P("rs", "pq"))
    return jax.shard_map(
        on_device, mesh=mesh, in_specs=placed, out_specs=P("pq", "rs", None), check_vma=False
    )
```

profile of v0, /device:TPU:1, one launch (start us, length us, event | category | flops | bytes accessed | tf_op | source)
XLA Modules:
  0.0 255.1 jit_solution(5755505084666371884)
XLA Ops:
  0.0 0.7 broadcast_in_dim.6
  0.7 20.4 %all_to_all.25 = bf16[8,36,112]{2,1,0:T(8,128)(2,1)S(1)} all-to-all(bf16[8,36,112]{2,1,0:T(8,128)(2,1)S(1)} %broadcast_in_dim.6), channel_id=1, replica_groups=mesh['pq'=8,'rs'=32] {'pq'}, dimensions={0} | all-to-all | bytes 129024 | tf_op jit(solution)/shard_map/all_to_all | solution.py:18
  21.1 0.1 broadcast_in_dim.14
  21.3 1.6 broadcast_in_dim.15
  22.8 8.1 %all-to-all-start.1 = ((bf16[32,36,896]{2,1,0:T(8,128)(2,1)}), bf16[32,36,896]{2,1,0:T(8,128)(2,1)S(1)}, u32[]{:S(2)}, u32[]{:S(2)}) async-start(bf16[32,36,896]{2,1,0:T(8,128)(2,1)} %broadcast_in_dim.15), calls=%async_computation.1 | async-start | bytes 4587520 | tf_op jit(solution)/shard_map/all_to_all | solution.py:18
  30.9 8.0 %copy.15 = bf16[64,36,1152]{2,1,0:T(8,128)(2,1)} copy(bf16[64,36,1152]{2,0,1:T(8,128)(2,1)} %param.2) | data formatting | bytes 10616832 | tf_op args[0]
  39.0 8.9 %reshape.11 = bf16[2304,1152]{1,0:T(8,128)(2,1)} reshape(bf16[64,36,1152]{2,1,0:T(8,128)(2,1)} %copy.15) | data formatting | bytes 10616832 | tf_op jit(solution)/shard_map/reshape | solution.py:36
  47.8 37.1 %all-to-all-done.1 = bf16[32,36,896]{2,1,0:T(8,128)(2,1)S(1)} async-done(((bf16[32,36,896]{2,1,0:T(8,128)(2,1)}), bf16[32,36,896]{2,1,0:T(8,128)(2,1)S(1)}, u32[]{:S(2)}, u32[]{:S(2)}) %all-to-all-start.1) | async-done | bytes 2064416 | tf_op jit(solution)/shard_map/all_to_all | solution.py:18
  84.9 1.9 reshape.12
  86.9 10.0 %convolution_convert_fusion = bf16[2304,896]{1,0:T(8,128)(2,1)} fusion(bf16[2304,1152]{1,0:T(8,128)(2,1)} %reshape.11, bf16[1152,896]{1,0:T(8,128)(2,1)} %reshape.12), kind=kOutput, calls=%fused_computation.4 | convolution fusion | flops 4758405120 | bytes 11501568 | tf_op jit(solution)/shard_map/dot_general | solution.py:39
  96.8 6.9 %reshape.13 = bf16[64,36,896]{2,1,0:T(8,128)(2,1)} reshape(bf16[2304,896]{1,0:T(8,128)(2,1)} %convolution_convert_fusion) | data formatting | bytes 8257536 | tf_op jit(solution)/shard_map/reshape | solution.py:40
  103.7 13.9 %copy.17 = bf16[64,36,896]{0,1,2:T(8,128)(2,1)} copy(bf16[64,36,896]{2,1,0:T(8,128)(2,1)} %reshape.13) | data formatting | bytes 8257536 | tf_op jit(solution)/shard_map/reshape | solution.py:40
  117.6 13.7 %reshape.16 = bf16[32,2,32256]{2,1,0:T(2,128)(2,1)} reshape(bf16[896,36,64]{2,1,0:T(8,128)(2,1)} %bitcast.18) | data formatting | bytes 8257536
  131.3 99.3 %all_to_all.26 = bf16[32,2,32256]{2,1,0:T(2,128)(2,1)} all-to-all(bf16[32,2,32256]{2,1,0:T(2,128)(2,1)} %reshape.16), channel_id=1, replica_groups=mesh['pq'=8,'rs'=32] {'rs'}, dimensions={0} | all-to-all | bytes 8257536 | tf_op jit(solution)/shard_map/all_to_all | solution.py:41
  230.6 14.6 %reshape.17 = bf16[896,36,64]{2,1,0:T(8,128)(2,1)} reshape(bf16[32,2,32256]{2,1,0:T(2,128)(2,1)} %all_to_all.26) | data formatting | bytes 8257536
  245.2 9.9 %bitcast_convert_fusion = bf16[64,28,896]{2,0,1:T(8,128)(2,1)} fusion(bf16[64,36,32,28]{0,1,3,2:T(8,128)(2,1)} %bitcast.17, bf16[32,36,896]{2,1,0:T(8,128)(2,1)S(1)} %all-to-all-done.1), kind=kOutput, calls=%fused_computation.3 | convolution fusion | flops 3700981760 | bytes 9404416 | tf_op jit(solution)/shard_map/prl,rk->plk/dot_general | solution.py:28
  (1 shorter events, 0.0 us)
Async XLA Ops:
  22.8 62.1 %all-to-all-start.1 = ((bf16[32,36,896]{2,1,0:T(8,128)(2,1)}), bf16[32,36,896]{2,1,0:T(8,128)(2,1)S(1)}, u32[]{:S(2)}, u32[]{:S(2)}) async-start(bf16[32,36,896]{2,1,0:T(8,128)(2,1)} %broadcast_in_dim.15), calls=%async_computation.1 | async-start | bytes 4587520 | tf_op jit(solution)/shard_map/all_to_all | solution.py:18
where the time goes:
time: 257 us; the launch traced here: 255 us
  blocking collectives  120 us (47%)
  local copies, waits for them, and re-layouts  70.4 us (27%)
  waiting for transfers between devices  37.1 us (14%)
  matrix products  19.8 us (8%)
  starting transfers between devices  8.09 us (3%)
    all_to_all x1, blocking collectives, on_device(): lax.all_to_all(first, 'rs', split_axis=2, concat_axis=1, tiled=True)  99.3 us
    all_to_all x1, waiting for transfers between devices, from_everyone(): lax.all_to_all(jnp.broadcast_to(array[None], (count, *array.shape)), axis...  37.1 us
    unnamed x3, local copies, waits for them, and re-layouts  36.4 us
    reshape x2, local copies, waits for them, and re-layouts, on_device(): first = first.reshape(pair_rows, block_rows, NORB)  20.8 us
    all_to_all x1, blocking collectives, from_everyone(): lax.all_to_all(jnp.broadcast_to(array[None], (count, *array.shape)), axis...  20.4 us
    dot_general x1, matrix products, on_device(): jnp.dot(flat, panel, preferred_element_type=jnp.float32)  9.95 us
    dot_general x1, matrix products, second_half(): jnp.einsum('prl,rk->plk', received, panel, preferred_element_type=jnp.flo...  9.88 us
    reshape x1, local copies, waits for them, and re-layouts, on_device(): flat = integrals.reshape(pair_rows * block_rows, NBASIS)  8.88 us
  transfers between devices with their start and end apart: 1, of which 1 were waited for; matrix products, arithmetic and copies ran while one was open for 7% of the time, Pallas kernels for 0%

commit v1 on v0

--- a/solution.py
+++ b/solution.py
@@ -38,7 +38,13 @@
     panel = collect(strip, "rs", 0)
     first = jnp.dot(flat, panel, preferred_element_type=jnp.float32).astype(jnp.bfloat16)
     first = first.reshape(pair_rows, block_rows, NORB)
-    return second_half(lax.all_to_all(first, "rs", split_axis=2, concat_axis=1, tiled=True), panel)
+    return second_half(
+        jnp.concatenate(
+            lax.all_to_all(jnp.stack(jnp.split(first, lax.axis_size("rs"), axis=2)), "rs", 0, 0),
+            axis=1,
+        ),
+        panel,
+    )
 
 
 def solution(mesh):

time: 257 us -> 320 us (1.25)
  local copies, waits for them, and re-layouts: 70.4 us -> 133 us
    unnamed x3 -> x38, local copies, waits for them, and re-layouts: 36.4 us -> 88.4 us
    another operation x0 -> x2, local copies, waits for them, and re-layouts: none -> 24.5 us  [on_device(): jnp.stack(jnp.split(first, lax.axis_size('rs'), axis=2))]
    reshape x2 -> x1, local copies, waits for them, and re-layouts: 20.8 us -> 6.94 us  [on_device(): first = first.reshape(pair_rows, block_rows, NORB)]
  transfers between devices with their start and end apart: 1 -> 1, of which waited for: 1 -> 1; matrix products, arithmetic and copies ran while one was open for 7% -> 5% of each run, Pallas kernels for 0% -> 0%
where the time goes in v1:
time: 320 us; the launch traced here: 318 us
  local copies, waits for them, and re-layouts  133 us (42%)
  blocking collectives  120 us (38%)
  waiting for transfers between devices  37 us (12%)
  matrix products  19.9 us (6%)
  starting transfers between devices  8.09 us (3%)
    all_to_all x1, blocking collectives, on_device(): lax.all_to_all(jnp.stack(jnp.split(first, lax.axis_size('rs'), axis=2)),...  99.3 us
    unnamed x38, local copies, waits for them, and re-layouts  88.4 us
    all_to_all x1, waiting for transfers between devices, from_everyone(): lax.all_to_all(jnp.broadcast_to(array[None], (count, *array.shape)), axis...  37 us
    another operation x2, local copies, waits for them, and re-layouts, on_device(): jnp.stack(jnp.split(first, lax.axis_size('rs'), axis=2))  24.5 us
    all_to_all x1, blocking collectives, from_everyone(): lax.all_to_all(jnp.broadcast_to(array[None], (count, *array.shape)), axis...  20.4 us
    dot_general x1, matrix products, on_device(): jnp.dot(flat, panel, preferred_element_type=jnp.float32)  9.96 us
    dot_general x1, matrix products, second_half(): jnp.einsum('prl,rk->plk', received, panel, preferred_element_type=jnp.flo...  9.96 us
    reshape x1, local copies, waits for them, and re-layouts, on_device(): flat = integrals.reshape(pair_rows * block_rows, NBASIS)  8.91 us
  transfers between devices with their start and end apart: 1, of which 1 were waited for; matrix products, arithmetic and copies ran while one was open for 5% of the time, Pallas kernels for 0%

profile of v1, /device:TPU:1, one launch (start us, length us, event | category | flops | bytes accessed | tf_op | source)
XLA Modules:
  0.0 318.0 jit_solution(9949122319314009600)
XLA Ops:
  0.0 0.7 broadcast_in_dim.6
  0.7 20.4 %all_to_all.15 = bf16[8,36,112]{2,1,0:T(8,128)(2,1)S(1)} all-to-all(bf16[8,36,112]{2,1,0:T(8,128)(2,1)S(1)} %broadcast_in_dim.6), channel_id=1, replica_groups=mesh['pq'=8,'rs'=32] {'pq'}, dimensions={0} | all-to-all | bytes 129024 | tf_op jit(solution)/shard_map/all_to_all | solution.py:18
  21.1 0.1 broadcast_in_dim.14
  21.3 1.6 broadcast_in_dim.15
  22.8 8.1 %all-to-all-start.1 = ((bf16[32,36,896]{2,1,0:T(8,128)(2,1)}), bf16[32,36,896]{2,1,0:T(8,128)(2,1)S(1)}, u32[]{:S(2)}, u32[]{:S(2)}) async-start(bf16[32,36,896]{2,1,0:T(8,128)(2,1)} %broadcast_in_dim.15), calls=%async_computation.1 | async-start | bytes 4587520 | tf_op jit(solution)/shard_map/all_to_all | solution.py:18
  30.9 8.0 %copy.109 = bf16[64,36,1152]{2,1,0:T(8,128)(2,1)} copy(bf16[64,36,1152]{2,0,1:T(8,128)(2,1)} %param.2) | data formatting | bytes 10616832 | tf_op args[0]
  39.0 8.9 %reshape.15 = bf16[2304,1152]{1,0:T(8,128)(2,1)} reshape(bf16[64,36,1152]{2,1,0:T(8,128)(2,1)} %copy.109) | data formatting | bytes 10616832 | tf_op jit(solution)/shard_map/reshape | solution.py:36
  47.9 37.0 %all-to-all-done.1 = bf16[32,36,896]{2,1,0:T(8,128)(2,1)S(1)} async-done(((bf16[32,36,896]{2,1,0:T(8,128)(2,1)}), bf16[32,36,896]{2,1,0:T(8,128)(2,1)S(1)}, u32[]{:S(2)}, u32[]{:S(2)}) %all-to-all-start.1) | async-done | bytes 2064416 | tf_op jit(solution)/shard_map/all_to_all | solution.py:18
  84.9 1.9 reshape.16
  86.9 10.0 %convolution_convert_fusion = bf16[2304,896]{1,0:T(8,128)(2,1)} fusion(bf16[2304,1152]{1,0:T(8,128)(2,1)} %reshape.15, bf16[1152,896]{1,0:T(8,128)(2,1)} %reshape.16), kind=kOutput, calls=%fused_computation.3 | convolution fusion | flops 4758405120 | bytes 11501568 | tf_op jit(solution)/shard_map/dot_general | solution.py:39
  96.8 6.9 %reshape.17 = bf16[64,36,896]{2,1,0:T(8,128)(2,1)} reshape(bf16[2304,896]{1,0:T(8,128)(2,1)} %convolution_convert_fusion) | data formatting | bytes 8257536 | tf_op jit(solution)/shard_map/reshape | solution.py:40
  103.8 0.0 slice-start
  103.8 2.1 fusion.36
  105.9 2.2 fusion.35
  108.1 2.2 fusion.34
  110.3 2.2 fusion.33
  112.4 2.4 fusion.32
  114.8 2.2 fusion.31
  117.0 2.2 fusion.30
  119.2 2.2 fusion.29
  121.3 0.0 slice-start.1
  121.3 2.3 fusion.28
  123.6 2.4 fusion.27
  126.0 2.2 fusion.26
  128.2 2.1 fusion.25
  130.4 2.2 fusion.24
  132.6 2.5 fusion.23
  135.1 2.2 fusion.22
  137.2 2.1 fusion.21
  139.4 0.0 slice-done
  139.4 0.0 slice-done.1
  139.4 1.1 fusion.20
  140.5 1.1 fusion.19
  141.5 1.1 fusion.18
  142.6 1.1 fusion.17
  143.8 1.1 fusion.16
  144.9 1.1 fusion.15
  146.0 1.1 fusion.14
  147.1 1.1 fusion.13
  148.2 1.1 fusion.12
  149.3 1.1 fusion.11
  150.4 1.1 fusion.10
  151.5 1.1 fusion.9
  152.6 1.1 fusion.8
  153.7 1.1 fusion.7
  154.8 1.1 fusion.6
  155.9 1.1 fusion.5
  156.9 23.5 %copy.111 = bf16[32,64,36,28]{1,2,3,0:T(8,128)(2,1)} copy(bf16[32,64,36,28]{3,2,1,0:T(8,128)(2,1)} %fusion.5) | data formatting | bytes 8257536 | tf_op jit(solution)/shard_map/stack | solution.py:43
  180.4 13.7 %reshape.21 = bf16[32,2,32256]{2,1,0:T(2,128)(2,1)} reshape(bf16[32,28,36,64]{3,2,1,0:T(8,128)(2,1)} %bitcast.151) | data formatting | bytes 8257536
  194.1 99.3 %all_to_all.16 = bf16[32,2,32256]{2,1,0:T(2,128)(2,1)} all-to-all(bf16[32,2,32256]{2,1,0:T(2,128)(2,1)} %reshape.21), channel_id=1, replica_groups=mesh['pq'=8,'rs'=32] {'rs'}, dimensions={0} | all-to-all | bytes 8257536 | tf_op jit(solution)/shard_map/all_to_all | solution.py:43
  293.4 14.6 %reshape.22 = bf16[32,28,36,64]{3,2,1,0:T(8,128)(2,1)} reshape(bf16[32,2,32256]{2,1,0:T(2,128)(2,1)} %all_to_all.16) | data formatting | bytes 8257536
  308.0 10.0 %bitcast_convert_fusion = bf16[64,28,896]{2,0,1:T(8,128)(2,1)} fusion(bf16[32,36,896]{2,1,0:T(8,128)(2,1)S(1)} %all-to-all-done.1, bf16[32,28,36,64]{3,2,1,0:T(8,128)(2,1)} %reshape.22), kind=kOutput, calls=%fused_computation.2 | convolution fusion | flops 3700981760 | bytes 9404416 | tf_op jit(solution)/shard_map/prl,rk->plk/dot_general | solution.py:28
  (2 shorter events, 0.0 us)
Async XLA Ops:
  22.8 62.1 %all-to-all-start.1 = ((bf16[32,36,896]{2,1,0:T(8,128)(2,1)}), bf16[32,36,896]{2,1,0:T(8,128)(2,1)S(1)}, u32[]{:S(2)}, u32[]{:S(2)}) async-start(bf16[32,36,896]{2,1,0:T(8,128)(2,1)} %broadcast_in_dim.15), calls=%async_computation.1 | async-start | bytes 4587520 | tf_op jit(solution)/shard_map/all_to_all | solution.py:18
  103.8 35.6 %slice-start = ((s8[4587520]{0:T(1024)(128)(4,1)}), s8[4194304]{0:T(1024)(128)(4,1)S(1)}, s32[]{:S(2)}) async-start(s8[4587520]{0:T(1024)(128)(4,1)} %bitcast.149), calls=%async_computation.3 | async-start | bytes 8388608
  121.3 18.0 %slice-start.1 = ((s8[4587520]{0:T(1024)(128)(4,1)}), s8[393216]{0:T(1024)(128)(4,1)S(1)}, s32[]{:S(2)}) async-start(s8[4587520]{0:T(1024)(128)(4,1)} %bitcast.149), calls=%async_computation.4 | async-start | bytes 786432
